TPU v7x, 128 devices: a whole 4x4x4 slice. The times are simulated.
128 devices in a mesh: seq: 16 (over z_lo, x, core), slate: 8 (over y, z_hi).
Axes of the slice: x: 4, y: 4, z: 4 (z_hi: 2, z_lo: 2; z = z_hi * 2 + z_lo), core: 2. Of those that a mesh axis runs over, the one named last changes fastest.
Arguments:
- features: bfloat16 [8, 12288, 512], P('slate', 'seq'), may hold values from -6 to 6
- user_ids: int32 [8], P('slate'), may hold values from 0 to 1023
- labels: int32 [8, 12288], P('slate', 'seq'), may hold values from 0 to 4, as said below
- user_table: bfloat16 [1024, 512], replicated, may hold values from -3 to 3
- gain_in: float32 [512], replicated, may hold values from 0.5 to 1.5
- w_query: bfloat16 [512, 512], replicated, may hold values from -0.75 to 0.75
- w_key: bfloat16 [512, 512], replicated, may hold values from -0.75 to 0.75
- w_value: bfloat16 [512, 512], replicated, may hold values from -0.25 to 0.25
- w_out: bfloat16 [512, 512], replicated, may hold values from -0.25 to 0.25
- gain_out: float32 [512], replicated, may hold values from 0.5 to 1.5
- w_score: float32 [512], replicated, may hold values from -0.25 to 0.25
Outputs:
- mixed: bfloat16 [8, 12288, 512], P('slate', 'seq')
- scores: float32 [8, 12288], P('slate', 'seq')
- loss: float32 [], replicated
Inputs may be any that keep to these rules, and one draw needn't show every extreme that they name: `labels`: relevance grades of the items.
All inputs are finite; a program needn't handle non-finite values.
Results may differ from a plain program's by a relative error of at most 0.0045.
Values may be sent and summed in bfloat16 or wider, within the bound.
A program may use at most 192 MiB of HBM per device.

v0:
```python
import math

import jax
import jax.numpy as jnp
from jax import lax
from jax.sharding import PartitionSpec as P

HEADS = 8


soft_cap = 20.0
norm_eps = 1e-06


def sent_to_all(shard, axis):
    copies = jnp.broadcast_to(shard, (lax.axis_size(axis), *shard.shape))
    return lax.all_to_all(copies, axis, split_axis=0, concat_axis=0, tiled=True)


def taken_together(shard, axis):
    return sent_to_all(shard, axis).sum(axis=0)


def in_one(arrays, axis):
    ends = [0]
    for a in arrays:
        ends.append(ends[-1] + a.size)
    running = taken_together(jnp.concatenate([a.ravel() for a in arrays]), axis)
    return tuple((running[b:e].reshape(a.shape) for a, b, e in zip(arrays, ends, ends[1:])))


def rms_norm(inputs_row, gain_row):
    return (
        inputs_row
        * lax.rsqrt(jnp.mean(inputs_row * inputs_row, axis=-1, keepdims=True) + norm_eps)
        * gain_row
    )


def shards(
    features,
    user_ids,
    labels,
    user_table,
    gain_in,
    w_query,
    w_key,
    w_value,
    w_out,
    gain_out,
    w_score,
):
    local_items = features[0]
    item_rows = local_items.shape[0]
    model_width = local_items.shape[1]
    head_dim = model_width // HEADS
    score_scale = 1.0 / math.sqrt(head_dim)
    slate_items = float(item_rows * lax.axis_size("seq"))
    one_hot = (jnp.arange(user_table.shape[0], dtype=jnp.int32) == user_ids[0]).astype(
        jnp.bfloat16
    )[None, :]
    personal = jnp.dot(one_hot, user_table, preferred_element_type=jnp.float32)
    hidden = local_items.astype(jnp.float32) + personal
    normed = rms_norm(hidden, gain_in).astype(jnp.bfloat16)
    queries = jnp.dot(normed, w_query, preferred_element_type=jnp.float32).astype(jnp.bfloat16)
    query_heads = jnp.transpose(queries.reshape(item_rows, HEADS, head_dim), (1, 0, 2))

    def absorb(running, keys_part, values_part):
        weighted, totals = running
        key_heads = keys_part.reshape(keys_part.shape[0], HEADS, head_dim)
        value_heads = values_part.reshape(values_part.shape[0], HEADS, head_dim)
        logits = (
            jnp.einsum("hqd,khd->hqk", query_heads, key_heads, preferred_element_type=jnp.float32)
            * score_scale
        )
        exp_scores = jnp.exp(soft_cap * jnp.tanh(logits / soft_cap))
        totals = totals + jnp.sum(exp_scores, axis=-1)
        weighted = weighted + jnp.einsum(
            "hqk,khd->qhd",
            exp_scores.astype(jnp.bfloat16),
            value_heads,
            preferred_element_type=jnp.float32,
        )
        return (weighted, totals)

    initial = (
        jnp.zeros((item_rows, HEADS, head_dim), jnp.float32),
        jnp.zeros((HEADS, item_rows), jnp.float32),
    )
    segment = lax.all_gather(normed, "seq", axis=0, tiled=True)
    keys_rows = jnp.dot(segment, w_key, preferred_element_type=jnp.float32).astype(jnp.bfloat16)
    values_rows = jnp.dot(segment, w_value, preferred_element_type=jnp.float32).astype(jnp.bfloat16)
    seg_rows = keys_rows.shape[0]
    stacked = (
        keys_rows.reshape(seg_rows // item_rows, item_rows, model_width),
        values_rows.reshape(seg_rows // item_rows, item_rows, model_width),
    )

    def visitor(inner_run, key_value):
        return (absorb(inner_run, key_value[0], key_value[1]), None)

    weighted, totals = lax.scan(visitor, initial, stacked)[0]
    attended = (
        (weighted / jnp.transpose(totals)[:, :, None])
        .reshape(item_rows, model_width)
        .astype(jnp.bfloat16)
    )
    mixed_sum = hidden + jnp.dot(attended, w_out, preferred_element_type=jnp.float32)
    out_normed = rms_norm(mixed_sum, gain_out)
    scored = jnp.sum(out_normed * w_score, axis=-1)
    label_weight = jnp.exp(labels[0].astype(jnp.float32))
    exp_part = jnp.sum(jnp.exp(scored))
    weight_part = jnp.sum(label_weight)
    product_part = jnp.sum(label_weight * scored)
    partition, weight_sum, weighted_score = in_one((exp_part, weight_part, product_part), "seq")
    total_loss = taken_together(
        jnp.log(partition / slate_items) - weighted_score / weight_sum, "slate"
    )
    return (mixed_sum.astype(jnp.bfloat16)[None], scored[None], total_loss)


def solution(mesh):
    return jax.shard_map(
        shards,
        mesh=mesh,
        in_specs=(
            P("slate", "seq", None),
            P("slate"),
            P("slate", "seq"),
            P(),
            P(),
            P(),
            P(),
            P(),
            P(),
            P(),
            P(),
        ),
        out_specs=(P("slate", "seq", None), P("slate", "seq"), P()),
        check_vma=False,
    )
```

profile of v0, /device:TPU:0, one launch (start us, length us, event | category | flops | bytes accessed | tf_op | source)
XLA Modules:
  0.0 513.7 jit_solution(11579012823203197518)
XLA Ops:
  14.5 71.2 %all-gather.2.cloned.1.call-done = bf16[12288,512]{0,1:T(8,128)(2,1)} async-done(((bf16[768,512]{0,1:T(8,128)(2,1)}), bf16[12288,512]{0,1:T(8,128)(2,1)}) %all-gather.2.cloned.1.call-update) | async-done | bytes 12582928 | tf_op jit(solution)/shard_map/all_gather | solution.py:90
  85.7 14.5 %convolution_convert_fusion.1 = bf16[12288,512]{1,0:T(8,128)(2,1)} fusion(bf16[12288,512]{0,1:T(8,128)(2,1)} %all-gather.2.cloned.1.call-done, bf16[512,512]{1,0:T(8,128)(2,1)S(1)} %copy-done.10), kind=kOutput, calls=%fused_computation.11 | convolution fusion | flops 6448742400 | bytes 25690112 | tf_op jit(solution)/shard_map/dot_general | solution.py:92
  100.2 9.9 %convolution_convert_fusion = bf16[12288,512]{1,0:T(8,128)(2,1)} fusion(bf16[12288,512]{0,1:T(8,128)(2,1)S(1)} %copy-done.8, bf16[512,512]{1,0:T(8,128)(2,1)S(1)} %copy-done.11), kind=kOutput, calls=%fused_computation.10 | convolution fusion | flops 6448742400 | bytes 25690112 | tf_op jit(solution)/shard_map/dot_general | solution.py:91
  110.1 363.0 %while.15 = (s32[]{:T(128)}, f32[768,8,64]{0,2,1:T(8,128)S(1)}, f32[8,768]{1,0:T(8,128)S(1)}, bf16[16,768,512]{2,1,0:T(8,128)(2,1)}, bf16[16,768,512]{2,1,0:T(8,...) while((s32[]{:T(128)}, f32[768,8,64]{0,2,1:T(8,128)S(1)}, ...), condition=%wide.region_3.4_spmd.clone, body=%wide.region_1.3_spmd.clone.sunk | while | flops 1237063680 | bytes 49643616 | solution.py:102
  112.7 10.4 %bitcast_reduce_fusion.2 = (f32[8,768]{1,0:T(8,128)S(1)}, f32[8,768,768]{2,1,0:T(8,128)}) fusion(bf16[768,8,64]{0,2,1:T(8,128)(2,1)} %bitcast.61, bf16[8,768,64]{1,2,0:T(8,128)(2,1)} %get-tuple-element.233), kind=kOutput, calls=%fused_computation.clone.1 | convolution fusion | flops 618129408 | bytes 20471808 | tf_op jit(solution)/shard_map/while/body/eval_jaxpr/hqd,khd->hqk/dot_general | solution.py:73
  135.4 10.4 %bitcast_reduce_fusion.2 = (f32[8,768]{1,0:T(8,128)S(1)}, f32[8,768,768]{2,1,0:T(8,128)}) fusion(bf16[768,8,64]{0,2,1:T(8,128)(2,1)} %bitcast.61, bf16[8,768,64]{1,2,0:T(8,128)(2,1)} %get-tuple-element.233), kind=kOutput, calls=%fused_computation.clone.1 | convolution fusion | flops 618129408 | bytes 20471808 | tf_op jit(solution)/shard_map/while/body/eval_jaxpr/hqd,khd->hqk/dot_general | solution.py:73
  158.1 10.4 %bitcast_reduce_fusion.2 = (f32[8,768]{1,0:T(8,128)S(1)}, f32[8,768,768]{2,1,0:T(8,128)}) fusion(bf16[768,8,64]{0,2,1:T(8,128)(2,1)} %bitcast.61, bf16[8,768,64]{1,2,0:T(8,128)(2,1)} %get-tuple-element.233), kind=kOutput, calls=%fused_computation.clone.1 | convolution fusion | flops 618129408 | bytes 20471808 | tf_op jit(solution)/shard_map/while/body/eval_jaxpr/hqd,khd->hqk/dot_general | solution.py:73
  168.8 9.3 %bitcast_add_fusion.2 = f32[768,8,64]{0,2,1:T(8,128)S(1)} fusion(f32[768,8,64]{0,2,1:T(8,128)S(1)} %get-tuple-element.221, bf16[768,8,64]{0,2,1:T(8,128)(2,1)S(1)} %bitcast.60, f32[8,768,768]{2,1,0:T(8,128)} %get-tuple-element.210, pred[]{:T(512)S(6)} %compare.3), kind=kOutput, calls=%fused_computation.4.clone.1 | convolution fusion | flops 618921984 | bytes 22806528 | tf_op jit(solution)/shard_map/while/body/eval_jaxpr/hqk,khd->qhd/dot_general | solution.py:78
  180.8 10.4 %bitcast_reduce_fusion.2 = (f32[8,768]{1,0:T(8,128)S(1)}, f32[8,768,768]{2,1,0:T(8,128)}) fusion(bf16[768,8,64]{0,2,1:T(8,128)(2,1)} %bitcast.61, bf16[8,768,64]{1,2,0:T(8,128)(2,1)} %get-tuple-element.233), kind=kOutput, calls=%fused_computation.clone.1 | convolution fusion | flops 618129408 | bytes 20471808 | tf_op jit(solution)/shard_map/while/body/eval_jaxpr/hqd,khd->hqk/dot_general | solution.py:73
  191.5 9.3 %bitcast_add_fusion.2 = f32[768,8,64]{0,2,1:T(8,128)S(1)} fusion(f32[768,8,64]{0,2,1:T(8,128)S(1)} %get-tuple-element.221, bf16[768,8,64]{0,2,1:T(8,128)(2,1)S(1)} %bitcast.60, f32[8,768,768]{2,1,0:T(8,128)} %get-tuple-element.210, pred[]{:T(512)S(6)} %compare.3), kind=kOutput, calls=%fused_computation.4.clone.1 | convolution fusion | flops 618921984 | bytes 22806528 | tf_op jit(solution)/shard_map/while/body/eval_jaxpr/hqk,khd->qhd/dot_general | solution.py:78
  203.5 10.4 %bitcast_reduce_fusion.2 = (f32[8,768]{1,0:T(8,128)S(1)}, f32[8,768,768]{2,1,0:T(8,128)}) fusion(bf16[768,8,64]{0,2,1:T(8,128)(2,1)} %bitcast.61, bf16[8,768,64]{1,2,0:T(8,128)(2,1)} %get-tuple-element.233), kind=kOutput, calls=%fused_computation.clone.1 | convolution fusion | flops 618129408 | bytes 20471808 | tf_op jit(solution)/shard_map/while/body/eval_jaxpr/hqd,khd->hqk/dot_general | solution.py:73
  214.2 9.3 %bitcast_add_fusion.2 = f32[768,8,64]{0,2,1:T(8,128)S(1)} fusion(f32[768,8,64]{0,2,1:T(8,128)S(1)} %get-tuple-element.221, bf16[768,8,64]{0,2,1:T(8,128)(2,1)S(1)} %bitcast.60, f32[8,768,768]{2,1,0:T(8,128)} %get-tuple-element.210, pred[]{:T(512)S(6)} %compare.3), kind=kOutput, calls=%fused_computation.4.clone.1 | convolution fusion | flops 618921984 | bytes 22806528 | tf_op jit(solution)/shard_map/while/body/eval_jaxpr/hqk,khd->qhd/dot_general | solution.py:78
  226.1 10.4 %bitcast_reduce_fusion.2 = (f32[8,768]{1,0:T(8,128)S(1)}, f32[8,768,768]{2,1,0:T(8,128)}) fusion(bf16[768,8,64]{0,2,1:T(8,128)(2,1)} %bitcast.61, bf16[8,768,64]{1,2,0:T(8,128)(2,1)} %get-tuple-element.233), kind=kOutput, calls=%fused_computation.clone.1 | convolution fusion | flops 618129408 | bytes 20471808 | tf_op jit(solution)/shard_map/while/body/eval_jaxpr/hqd,khd->hqk/dot_general | solution.py:73
  248.8 10.4 %bitcast_reduce_fusion.2 = (f32[8,768]{1,0:T(8,128)S(1)}, f32[8,768,768]{2,1,0:T(8,128)}) fusion(bf16[768,8,64]{0,2,1:T(8,128)(2,1)} %bitcast.61, bf16[8,768,64]{1,2,0:T(8,128)(2,1)} %get-tuple-element.233), kind=kOutput, calls=%fused_computation.clone.1 | convolution fusion | flops 618129408 | bytes 20471808 | tf_op jit(solution)/shard_map/while/body/eval_jaxpr/hqd,khd->hqk/dot_general | solution.py:73
  271.5 10.4 %bitcast_reduce_fusion.2 = (f32[8,768]{1,0:T(8,128)S(1)}, f32[8,768,768]{2,1,0:T(8,128)}) fusion(bf16[768,8,64]{0,2,1:T(8,128)(2,1)} %bitcast.61, bf16[8,768,64]{1,2,0:T(8,128)(2,1)} %get-tuple-element.233), kind=kOutput, calls=%fused_computation.clone.1 | convolution fusion | flops 618129408 | bytes 20471808 | tf_op jit(solution)/shard_map/while/body/eval_jaxpr/hqd,khd->hqk/dot_general | solution.py:73
  294.2 10.4 %bitcast_reduce_fusion.2 = (f32[8,768]{1,0:T(8,128)S(1)}, f32[8,768,768]{2,1,0:T(8,128)}) fusion(bf16[768,8,64]{0,2,1:T(8,128)(2,1)} %bitcast.61, bf16[8,768,64]{1,2,0:T(8,128)(2,1)} %get-tuple-element.233), kind=kOutput, calls=%fused_computation.clone.1 | convolution fusion | flops 618129408 | bytes 20471808 | tf_op jit(solution)/shard_map/while/body/eval_jaxpr/hqd,khd->hqk/dot_general | solution.py:73
  316.9 10.4 %bitcast_reduce_fusion.2 = (f32[8,768]{1,0:T(8,128)S(1)}, f32[8,768,768]{2,1,0:T(8,128)}) fusion(bf16[768,8,64]{0,2,1:T(8,128)(2,1)} %bitcast.61, bf16[8,768,64]{1,2,0:T(8,128)(2,1)} %get-tuple-element.233), kind=kOutput, calls=%fused_computation.clone.1 | convolution fusion | flops 618129408 | bytes 20471808 | tf_op jit(solution)/shard_map/while/body/eval_jaxpr/hqd,khd->hqk/dot_general | solution.py:73
  339.6 10.4 %bitcast_reduce_fusion.2 = (f32[8,768]{1,0:T(8,128)S(1)}, f32[8,768,768]{2,1,0:T(8,128)}) fusion(bf16[768,8,64]{0,2,1:T(8,128)(2,1)} %bitcast.61, bf16[8,768,64]{1,2,0:T(8,128)(2,1)} %get-tuple-element.233), kind=kOutput, calls=%fused_computation.clone.1 | convolution fusion | flops 618129408 | bytes 20471808 | tf_op jit(solution)/shard_map/while/body/eval_jaxpr/hqd,khd->hqk/dot_general | solution.py:73
  362.3 10.4 %bitcast_reduce_fusion.2 = (f32[8,768]{1,0:T(8,128)S(1)}, f32[8,768,768]{2,1,0:T(8,128)}) fusion(bf16[768,8,64]{0,2,1:T(8,128)(2,1)} %bitcast.61, bf16[8,768,64]{1,2,0:T(8,128)(2,1)} %get-tuple-element.233), kind=kOutput, calls=%fused_computation.clone.1 | convolution fusion | flops 618129408 | bytes 20471808 | tf_op jit(solution)/shard_map/while/body/eval_jaxpr/hqd,khd->hqk/dot_general | solution.py:73
  384.9 10.4 %bitcast_reduce_fusion.2 = (f32[8,768]{1,0:T(8,128)S(1)}, f32[8,768,768]{2,1,0:T(8,128)}) fusion(bf16[768,8,64]{0,2,1:T(8,128)(2,1)} %bitcast.61, bf16[8,768,64]{1,2,0:T(8,128)(2,1)} %get-tuple-element.233), kind=kOutput, calls=%fused_computation.clone.1 | convolution fusion | flops 618129408 | bytes 20471808 | tf_op jit(solution)/shard_map/while/body/eval_jaxpr/hqd,khd->hqk/dot_general | solution.py:73
  407.6 10.4 %bitcast_reduce_fusion.2 = (f32[8,768]{1,0:T(8,128)S(1)}, f32[8,768,768]{2,1,0:T(8,128)}) fusion(bf16[768,8,64]{0,2,1:T(8,128)(2,1)} %bitcast.61, bf16[8,768,64]{1,2,0:T(8,128)(2,1)} %get-tuple-element.233), kind=kOutput, calls=%fused_computation.clone.1 | convolution fusion | flops 618129408 | bytes 20471808 | tf_op jit(solution)/shard_map/while/body/eval_jaxpr/hqd,khd->hqk/dot_general | solution.py:73
  430.3 10.4 %bitcast_reduce_fusion.2 = (f32[8,768]{1,0:T(8,128)S(1)}, f32[8,768,768]{2,1,0:T(8,128)}) fusion(bf16[768,8,64]{0,2,1:T(8,128)(2,1)} %bitcast.61, bf16[8,768,64]{1,2,0:T(8,128)(2,1)} %get-tuple-element.233), kind=kOutput, calls=%fused_computation.clone.1 | convolution fusion | flops 618129408 | bytes 20471808 | tf_op jit(solution)/shard_map/while/body/eval_jaxpr/hqd,khd->hqk/dot_general | solution.py:73
  453.0 10.4 %bitcast_reduce_fusion.2 = (f32[8,768]{1,0:T(8,128)S(1)}, f32[8,768,768]{2,1,0:T(8,128)}) fusion(bf16[768,8,64]{0,2,1:T(8,128)(2,1)} %bitcast.61, bf16[8,768,64]{1,2,0:T(8,128)(2,1)} %get-tuple-element.233), kind=kOutput, calls=%fused_computation.clone.1 | convolution fusion | flops 618129408 | bytes 20471808 | tf_op jit(solution)/shard_map/while/body/eval_jaxpr/hqd,khd->hqk/dot_general | solution.py:73
  492.2 14.1 %all_to_all.12 = f32[8,1,1]{2,1,0:T(1,128)S(1)} all-to-all(f32[8,1,1]{2,1,0:T(1,128)S(1)} %broadcast_in_dim.30), channel_id=1, replica_groups=mesh['seq'=16,'slate'=8] {'slate'}, dimensions={0} | all-to-all | bytes 64 | tf_op jit(solution)/shard_map/all_to_all | solution.py:17
  (131 shorter events, 191.6 us)
Async XLA Ops:
  7.2 2.2 copy-start
  7.2 2.8 copy-start.5
  7.2 78.5 %all-gather.2.cloned.1.call-start = ((), (), s32[]{:S(2)}) async-start(), calls=%async_computation.2 | async-start | bytes 13369344 | tf_op jit(solution)/shard_map/all_gather | solution.py:90
  8.7 2.4 copy-start.2
  9.7 1.6 copy-start.4
  9.7 2.2 copy-start.9
  11.2 74.5 %copy-start.10 = (bf16[512,512]{1,0:T(8,128)(2,1)S(1)}, bf16[512,512]{1,0:T(8,128)(2,1)}, u32[]{:S(2)}) copy-start(bf16[512,512]{1,0:T(8,128)(2,1)} %param.20) | copy-start | bytes 1572868
  14.5 85.7 %copy-start.11 = (bf16[512,512]{1,0:T(8,128)(2,1)S(1)}, bf16[512,512]{1,0:T(8,128)(2,1)}, u32[]{:S(2)}) copy-start(bf16[512,512]{1,0:T(8,128)(2,1)} %param.19) | copy-start | bytes 1572868
  85.7 14.5 %copy-start.8 = (bf16[12288,512]{0,1:T(8,128)(2,1)S(1)}, bf16[12288,512]{0,1:T(8,128)(2,1)}, u32[]{:S(2)}) copy-start(bf16[12288,512]{0,1:T(8,128)(2,1)} %all-gather.2.cloned.1.call-done) | copy-start | bytes 37748740
  473.0 1.1 copy-start.3
  473.1 1.3 copy-start.12
  474.3 0.7 copy-start.6
  474.3 0.7 copy-start.7
  475.0 31.9 %copy-start.1 = (bf16[1024,512]{1,0:T(8,128)(2,1)S(1)}, bf16[1024,512]{1,0:T(8,128)(2,1)}, u32[]{:S(2)}) copy-start(bf16[1024,512]{1,0:T(8,128)(2,1)} %param.16) | copy-start | bytes 3145732
  478.6 10.9 %all-to-all-start = ((f32[16,1,3]{2,1,0:T(1,128)}), f32[16,1,3]{2,1,0:T(1,128)S(1)}, u32[]{:S(2)}, u32[]{:S(2)}) async-start(f32[16,1,3]{2,1,0:T(1,128)} %broadcast_in_dim.29), calls=%async_computation | async-start | bytes 16384 | tf_op jit(solution)/shard_map/all_to_all | solution.py:17
Sparse Core Ops, SparseCore 0:
  11.3 74.3 all-gather.1
where the time goes:
time: 515 us; the launch traced here: 514 us
  matrix products  344 us (67%)
  waiting for transfers between devices  75.4 us (15%)
  local copies, waits for them, and re-layouts  52.1 us (10%)
  between operations  16.9 us (3%)
  blocking collectives  14.1 us (3%)
  other arithmetic  5.94 us (1%)
    dot_general x16, matrix products, absorb(): jnp.einsum('hqd,khd->hqk', query_heads, key_heads, preferred_element_type...  167 us
    dot_general x16, matrix products, absorb(): jnp.einsum('hqk,khd->qhd', exp_scores.astype(jnp.bfloat16), value_heads,...  149 us
    all_gather x1, waiting for transfers between devices, shards(): segment = lax.all_gather(normed, 'seq', axis=0, tiled=True)  71.2 us
    dynamic_slice x48, local copies, waits for them, and re-layouts, shards(): weighted, totals = lax.scan(visitor, initial, stacked)[0]  46.4 us
    dot_general x1, matrix products, shards(): jnp.dot(segment, w_value, preferred_element_type=jnp.float32)  14.5 us
    all_to_all x1, blocking collectives, sent_to_all(): return lax.all_to_all(copies, axis, split_axis=0, concat_axis=0, tiled=True)  14.1 us
  transfers between devices with their start and end apart: 2, of which 2 were waited for; matrix products, arithmetic and copies ran while one was open for 1% of the time, Pallas kernels for 0%

commit v1 on v0

v1 whole, which is shorter than its diff:
```python
import math

import jax
import jax.numpy as jnp
from jax import lax
from jax.experimental import pallas as pl
from jax.experimental.pallas import tpu as pltpu
from jax.sharding import PartitionSpec as P

HEADS = 8
soft_cap = 20.0
norm_eps = 1e-06

bf16, f32 = jnp.bfloat16, jnp.float32
LOG2E = 1.4426950408889634
BLOCK = 256
AHEAD = 3


def sent_to_all(shard, axis):
    copies = jnp.broadcast_to(shard, (lax.axis_size(axis), *shard.shape))
    return lax.all_to_all(copies, axis, split_axis=0, concat_axis=0, tiled=True)


def taken_together(shard, axis):
    return sent_to_all(shard, axis).sum(axis=0)


def in_one(arrays, axis):
    ends = [0]
    for a in arrays:
        ends.append(ends[-1] + a.size)
    running = taken_together(jnp.concatenate([a.ravel() for a in arrays]), axis)
    return tuple((running[b:e].reshape(a.shape) for a, b, e in zip(arrays, ends, ends[1:])))


def rms_norm(inputs_row, gain_row):
    return (
        inputs_row
        * lax.rsqrt(jnp.mean(inputs_row * inputs_row, axis=-1, keepdims=True) + norm_eps)
        * gain_row
    )


def capped_weight(products):
    return jnp.exp2(jnp.tanh(products * (128.0 / 8 / soft_cap)) * (soft_cap * LOG2E))


def project_keys(rows, wk, k_ref):
    keys = jnp.dot(rows, wk, preferred_element_type=f32).astype(bf16)
    for pair in range(2):
        k_ref[pair] = keys[:, pair * 128 : (pair + 1) * 128]


def project_values(rows, wv_t, vt_ref):
    values_t = lax.dot_general(
        wv_t, rows, (((1,), (1,)), ((), ())), preferred_element_type=f32
    ).astype(bf16)
    for head in range(4):
        vt_ref[head, 0:64, :] = values_t[head * 64 : (head + 1) * 64]


def project_queries(rows, wq_t, qt_ref, at):
    queries_t = lax.dot_general(
        wq_t, rows, (((1,), (1,)), ((), ())), preferred_element_type=f32
    ).astype(bf16) * bf16(1.0 / 128)
    count = rows.shape[0]
    for head in range(4):
        mine, other = (head % 2) * 64, 64 - (head % 2) * 64
        qt_ref[head, mine : mine + 64, at : at + count] = queries_t[head * 64 : (head + 1) * 64]
        qt_ref[head, other : other + 64, at : at + count] = jnp.zeros((64, count), bf16)


def attend(k_ref, vt_ref, qt_ref, o_ref, heads, tiles):
    kts = k_ref.shape[1] // BLOCK
    work = [(h, t, b) for h in heads for t in tiles for b in range(kts)]
    ready = {}
    total = None
    for i in range(len(work) + AHEAD):
        if i < len(work):
            h, t, b = work[i]
            products = jnp.dot(
                k_ref[h // 2, b * BLOCK : (b + 1) * BLOCK],
                qt_ref[h, :, t * BLOCK : (t + 1) * BLOCK],
                preferred_element_type=f32,
            )
            ready[i] = capped_weight(products).astype(bf16)
        if i >= AHEAD:
            h, t, b = work[i - AHEAD]
            part = jnp.dot(
                vt_ref[h, :, b * BLOCK : (b + 1) * BLOCK],
                ready.pop(i - AHEAD),
                preferred_element_type=f32,
            )
            total = part if b == 0 else total + part
            if b == kts - 1:
                o_ref[h, :, t * BLOCK : (t + 1) * BLOCK] += total


def attention_kernel(own_ref, seg_ref, wq_ref, wk_ref, wv_ref, out_ref, k_ref, vt_ref, qt_ref, o_ref):
    step = pl.program_id(0)

    @pl.when(step == 0)
    def _():
        o_ref[...] = jnp.zeros_like(o_ref)
        row = lax.broadcasted_iota(jnp.int32, (16, vt_ref.shape[2]), 0)
        for head in range(4):
            vt_ref[head, 64:80, :] = jnp.where(row == 0, 1.0, 0.0).astype(bf16)
        for t in range(own_ref.shape[0] // BLOCK):
            project_queries(own_ref[t * BLOCK : (t + 1) * BLOCK], wq_ref[...], qt_ref, t * BLOCK)

    project_keys(seg_ref[...], wk_ref[...], k_ref)
    project_values(seg_ref[...], wv_ref[...], vt_ref)
    attend(k_ref, vt_ref, qt_ref, o_ref, range(4), range(qt_ref.shape[2] // BLOCK))

    @pl.when(step == pl.num_programs(0) - 1)
    def _():
        for head in range(4):
            out_ref[head * 64 : (head + 1) * 64] = (
                o_ref[head, 0:64] / o_ref[head, 64:65]
            ).astype(bf16)


def attention(own, seg, wq_t, wk, wv_t, rows):
    queries, width = own.shape
    chunks = seg.shape[0] // rows
    whole = lambda shape: pl.BlockSpec(shape, lambda i: (0, 0))
    return pl.pallas_call(
        attention_kernel,
        grid=(chunks,),
        out_shape=jax.ShapeDtypeStruct((width // 2, queries), bf16),
        in_specs=[
            whole(own.shape),
            pl.BlockSpec((rows, width), lambda i: (i, 0)),
            whole(wq_t.shape),
            whole(wk.shape),
            whole(wv_t.shape),
        ],
        out_specs=whole((width // 2, queries)),
        scratch_shapes=[
            pltpu.VMEM((2, rows, 128), bf16),
            pltpu.VMEM((4, 80, rows), bf16),
            pltpu.VMEM((4, 128, queries), bf16),
            pltpu.VMEM((4, 80, queries), f32),
        ],
        compiler_params=pltpu.CompilerParams(vmem_limit_bytes=48 * 2**20),
        name="attention",
    )(own, seg, wq_t, wk, wv_t)


def shards(
    features,
    user_ids,
    labels,
    user_table,
    gain_in,
    w_query,
    w_key,
    w_value,
    w_out,
    gain_out,
    w_score,
):
    local_items = features[0]
    item_rows, model_width = local_items.shape
    half = model_width // 2
    ring = lax.axis_size("seq")
    slate_items = float(item_rows * ring)
    me = lax.axis_index("seq")
    core = me % 2
    personal = lax.dynamic_slice_in_dim(user_table, user_ids[0], 1, 0)
    hidden = local_items.astype(f32) + personal.astype(f32)
    normed = rms_norm(hidden, gain_in).astype(bf16)
    segment = lax.all_gather(normed, "seq", axis=0, tiled=True)
    cut = lambda w: lax.dynamic_slice_in_dim(w, core * half, half, 1)
    own = lax.dynamic_slice_in_dim(segment, (me - core) * item_rows, 2 * item_rows, 0)
    mine_t = attention(own, segment, cut(w_query).T, cut(w_key), cut(w_value).T, item_rows)
    kept = lax.dynamic_slice_in_dim(mine_t, core * item_rows, item_rows, 1)
    given = lax.dynamic_slice_in_dim(mine_t, (1 - core) * item_rows, item_rows, 1)
    got = lax.ppermute(given, "seq", [(i, i ^ 1) for i in range(ring)])
    attended_t = jnp.where(
        core == 0, jnp.concatenate([kept, got], 0), jnp.concatenate([got, kept], 0)
    )
    mixed_sum = hidden + lax.dot_general(
        attended_t, w_out, (((0,), (0,)), ((), ())), preferred_element_type=f32
    )
    out_normed = rms_norm(mixed_sum, gain_out)
    scored = jnp.sum(out_normed * w_score, axis=-1)
    label_weight = jnp.exp(labels[0].astype(f32))
    exp_part = jnp.sum(jnp.exp(scored))
    weight_part = jnp.sum(label_weight)
    product_part = jnp.sum(label_weight * scored)
    partition, weight_sum, weighted_score = in_one((exp_part, weight_part, product_part), "seq")
    total_loss = taken_together(
        jnp.log(partition / slate_items) - weighted_score / weight_sum, "slate"
    )
    return (mixed_sum.astype(bf16)[None], scored[None], total_loss)


def solution(mesh):
    return jax.shard_map(
        shards,
        mesh=mesh,
        in_specs=(
            P("slate", "seq", None),
            P("slate"),
            P("slate", "seq"),
            P(),
            P(),
            P(),
            P(),
            P(),
            P(),
            P(),
            P(),
        ),
        out_specs=(P("slate", "seq", None), P("slate", "seq"), P()),
        check_vma=False,
    )
```

time: 515 us -> 229 us (0.44)
  matrix products: 344 us -> 0.71 us
  Pallas kernels: 0 us -> 97.6 us
  local copies, waits for them, and re-layouts: 52.1 us -> 4.67 us
    dot_general x37 -> x1, matrix products: 344 us -> 0.71 us  [shards(): lax.dot_general(attended_t, w_out, (((0,), (0,)), ((), ())), preferred_el...]
    pallas_call x0 -> x1, Pallas kernels: none -> 97.6 us  [attention(): pl.pallas_call(attention_kernel, grid=(chunks,), out_shape=jax.ShapeDtype...]
    dynamic_slice x48 -> x4, local copies, waits for them, and re-layouts: 46.4 us -> 1.63 us  [the longest x1 1.51 us: shards(): lax.dynamic_slice_in_dim(segment, (me - core) * item_rows, 2 * item_rows, 0)]
  transfers between devices with their start and end apart: 2 -> 3, of which waited for: 2 -> 3; matrix products, arithmetic and copies ran while one was open for 1% -> 1% of each run, Pallas kernels for 0% -> 0%
where the time goes in v1:
time: 229 us
  Pallas kernels  97.6 us (43%)
  waiting for transfers between devices  79.4 us (35%)
  between operations  16.9 us (7%)
  blocking collectives  14.1 us (6%)
  other arithmetic  9.79 us (4%)
  starting transfers between devices  5.33 us (2%)
  local copies, waits for them, and re-layouts  4.67 us (2%)
    pallas_call x1, Pallas kernels, attention(): pl.pallas_call(attention_kernel, grid=(chunks,), out_shape=jax.ShapeDtype...  97.6 us
    all_gather x1, waiting for transfers between devices, shards(): segment = lax.all_gather(normed, 'seq', axis=0, tiled=True)  73.5 us
    all_to_all x1, blocking collectives, sent_to_all(): return lax.all_to_all(copies, axis, split_axis=0, concat_axis=0, tiled=True)  14.1 us
    all_to_all x1, waiting for transfers between devices, sent_to_all(): return lax.all_to_all(copies, axis, split_axis=0, concat_axis=0, tiled=True)  5.35 us
    all_to_all x1, starting transfers between devices, sent_to_all(): return lax.all_to_all(copies, axis, split_axis=0, concat_axis=0, tiled=True)  4.97 us
  transfers between devices with their start and end apart: 3, of which 3 were waited for; matrix products, arithmetic and copies ran while one was open for 1% of the time, Pallas kernels for 0%

profile of v1, /device:TPU:0, one launch (start us, length us, event | category | flops | bytes accessed | tf_op | source)
XLA Modules:
  0.0 228.5 jit_solution(4763980589965132763)
XLA Ops:
  7.9 0.7 dynamic-slice_convert_fusion
  8.6 1.5 fusion.3
  10.1 2.3 fusion.5
  12.5 0.1 copy.33
  12.7 0.1 copy.34
  12.8 0.6 copy-done.2
  13.5 73.5 %all-gather.2.cloned.1.call-done.seg_ref = bf16[12288,512]{1,0:T(8,128)(2,1)} async-done(((bf16[768,512]{1,0:T(8,128)(2,1)}), bf16[12288,512]{1,0:T(8,128)(2,1)}) %all-gather.2.cloned.1.call-update) | async-done | bytes 12582928 | tf_op jit(solution)/shard_map/all_gather | solution.py:174
  86.9 1.5 constant_dynamic-slice_fusion.5.own_ref
  88.4 97.6 %attention.1 = bf16[256,1536]{1,0:T(8,128)(2,1)S(1)} custom-call(bf16[1536,512]{1,0:T(8,128)(2,1)S(1)} %constant_dynamic-slice_fusion.5.own_ref, bf16[12288,512]{1,0:T(8,128)(2,1)} %all-gather.2.cloned.1.call-done.seg_ref, bf16[256,512]{1,0:T(8,128)(2,1)S(1)} %bitcast.19, bf16[512,256]{1,0:T(8,128)(2,1)S(1)} %constant_dynamic-slice_fusion.3.wk_ref, ...), custom_call_target="tpu_custom_call" | custom-call | tf_op jit(solution)/shard_map/attention/pallas_call | solution.py:128
  186.2 0.3 collective-permute-start
  186.5 0.3 copy-done.5
  186.8 0.6 fusion.13
  187.4 0.6 collective-permute-done
  188.0 0.7 multiply_reduce_fusion.1
  188.7 1.3 multiply_reduce_fusion
  190.0 0.7 exponential_reduce_fusion
  190.7 2.1 pad_maximum_fusion
  192.8 0.6 broadcast_in_dim.19
  193.4 5.0 %all-to-all-start = ((f32[16,1,3]{2,1,0:T(1,128)}), f32[16,1,3]{2,1,0:T(1,128)S(1)}, u32[]{:S(2)}, u32[]{:S(2)}) async-start(f32[16,1,3]{2,1,0:T(1,128)} %broadcast_in_dim.19), calls=%async_computation | async-start | bytes 16384 | tf_op jit(solution)/shard_map/all_to_all | solution.py:22
  198.4 0.6 broadcast_in_dim.18
  199.0 5.3 %all-to-all-done = f32[16,1,3]{2,1,0:T(1,128)S(1)} async-done(((f32[16,1,3]{2,1,0:T(1,128)}), f32[16,1,3]{2,1,0:T(1,128)S(1)}, u32[]{:S(2)}, u32[]{:S(2)}) %all-to-all-start) | async-done | bytes 224 | tf_op jit(solution)/shard_map/all_to_all | solution.py:22
  204.3 0.7 fusion.15
  207.0 14.1 %all_to_all.12 = f32[8,1,1]{2,1,0:T(1,128)S(1)} all-to-all(f32[8,1,1]{2,1,0:T(1,128)S(1)} %broadcast_in_dim.20), channel_id=1, replica_groups=mesh['seq'=16,'slate'=8] {'slate'}, dimensions={0} | all-to-all | bytes 64 | tf_op jit(solution)/shard_map/all_to_all | solution.py:22
  221.1 0.6 reduce_sum.79
  (23 shorter events, 0.3 us)
Async XLA Ops:
  7.2 180.8 %copy-start = (bf16[512,512]{1,0:T(8,128)(2,1)S(1)}, bf16[512,512]{1,0:T(8,128)(2,1)}, u32[]{:S(2)}) copy-start(bf16[512,512]{1,0:T(8,128)(2,1)} %param.19) | copy-start | bytes 1572868
  7.2 79.7 %all-gather.2.cloned.1.call-start = ((), (), s32[]{:S(2)}) async-start(), calls=%async_computation.2 | async-start | bytes 13369344 | tf_op jit(solution)/shard_map/all_gather | solution.py:174
  8.6 3.8 %copy-start.3 = (bf16[512,512]{1,0:T(8,128)(2,1)S(1)}, bf16[512,512]{1,0:T(8,128)(2,1)}, u32[]{:S(2)}) copy-start(bf16[512,512]{1,0:T(8,128)(2,1)} %param.18) | copy-start | bytes 1572868
  8.6 3.8 %copy-start.4 = (bf16[512,512]{1,0:T(8,128)(2,1)S(1)}, bf16[512,512]{1,0:T(8,128)(2,1)}, u32[]{:S(2)}) copy-start(bf16[512,512]{1,0:T(8,128)(2,1)} %param.16) | copy-start | bytes 1572868
  12.4 1.0 copy-start.2
  186.1 0.7 copy-start.5
  186.1 1.9 copy-start.1
  186.2 1.8 collective-permute-start
  188.0 0.7 copy-start.6
  188.0 0.7 copy-start.7
  193.4 10.9 %all-to-all-start = ((f32[16,1,3]{2,1,0:T(1,128)}), f32[16,1,3]{2,1,0:T(1,128)S(1)}, u32[]{:S(2)}, u32[]{:S(2)}) async-start(f32[16,1,3]{2,1,0:T(1,128)} %broadcast_in_dim.19), calls=%async_computation | async-start | bytes 16384 | tf_op jit(solution)/shard_map/all_to_all | solution.py:22
Sparse Core Ops, SparseCore 0:
  12.6 74.3 all-gather.1

commit v2 on v1

v2 whole, which is shorter than its diff:
```python
import functools

import jax
import jax.numpy as jnp
from jax import lax
from jax.experimental import pallas as pl
from jax.experimental.pallas import tpu as pltpu
from jax.sharding import PartitionSpec as P

HEADS = 8
soft_cap = 20.0
norm_eps = 1e-06

bf16, f32 = jnp.bfloat16, jnp.float32
LOG2E = 1.4426950408889634
BLOCK = 256
AHEAD = 3
MESH = pl.DeviceIdType.MESH


def capped_weight(products):
    return jnp.exp2(jnp.tanh(products * (128.0 / 8 / soft_cap)) * (soft_cap * LOG2E))


def project_keys(rows, wk, k_ref):
    keys = jnp.dot(rows, wk, preferred_element_type=f32).astype(bf16)
    for pair in range(2):
        k_ref[pair] = keys[:, pair * 128 : (pair + 1) * 128]


def project_values(rows, wv_t, vt_ref):
    values_t = lax.dot_general(
        wv_t, rows, (((1,), (1,)), ((), ())), preferred_element_type=f32
    ).astype(bf16)
    for head in range(4):
        vt_ref[head, 0:64, :] = values_t[head * 64 : (head + 1) * 64]


def project_queries(rows, wq_t, qt_ref, at):
    queries_t = lax.dot_general(
        wq_t, rows, (((1,), (1,)), ((), ())), preferred_element_type=f32
    ).astype(bf16) * bf16(1.0 / 128)
    count = rows.shape[0]
    for head in range(4):
        mine, other = (head % 2) * 64, 64 - (head % 2) * 64
        qt_ref[head, mine : mine + 64, at : at + count] = queries_t[head * 64 : (head + 1) * 64]
        qt_ref[head, other : other + 64, at : at + count] = jnp.zeros((64, count), bf16)


def attend(k_ref, vt_ref, qt_ref, o_ref, heads, tiles):
    kts = k_ref.shape[1] // BLOCK
    work = [(h, t, b) for h in heads for t in tiles for b in range(kts)]
    ready = {}
    total = None
    for i in range(len(work) + AHEAD):
        if i < len(work):
            h, t, b = work[i]
            products = jnp.dot(
                k_ref[h // 2, b * BLOCK : (b + 1) * BLOCK],
                qt_ref[h, :, t * BLOCK : (t + 1) * BLOCK],
                preferred_element_type=f32,
            )
            ready[i] = capped_weight(products).astype(bf16)
        if i >= AHEAD:
            h, t, b = work[i - AHEAD]
            part = jnp.dot(
                vt_ref[h, :, b * BLOCK : (b + 1) * BLOCK],
                ready.pop(i - AHEAD),
                preferred_element_type=f32,
            )
            total = part if b == 0 else total + part
            if b == kts - 1:
                o_ref[h, :, t * BLOCK : (t + 1) * BLOCK] += total


def rms_scale(rows):
    return lax.rsqrt(jnp.mean(rows * rows, axis=-1, keepdims=True) + norm_eps)


def fused_kernel(
    seq,
    slates,
    features_ref,
    personal_ref,
    labels_ref,
    gain_in_ref,
    wq_ref,
    wk_ref,
    wv_ref,
    wo_ref,
    gain_out_ref,
    w_score_ref,
    mixed_ref,
    scores_ref,
    loss_ref,
    x_ref,
    k_ref,
    vt_ref,
    qt_ref,
    o_ref,
    give_ref,
    att_ref,
    wvt_ref,
    parts_ref,
    losses_ref,
    send_sem,
    recv_sem,
    parts_send,
    parts_recv,
    losses_send,
    losses_recv,
):
    rows, width = features_ref.shape
    half = width // 2
    third = rows // 3
    me = lax.axis_index("seq")
    my_slate = lax.axis_index("slate")
    core, x, z = lax.rem(me, 2), lax.rem(lax.div(me, 2), 4), lax.div(me, 8)
    at = lambda zz, xx, cc: (zz * 4 + xx) * 2 + cc
    right = at(z, lax.rem(x + 1, 4), core)
    left = at(z, lax.rem(x + 3, 4), core)
    across = at(1 - z, x, core)
    partner = at(z, x, 1 - core)

    barrier = pltpu.get_barrier_semaphore()
    for k in range(1, seq):
        pl.semaphore_signal(
            barrier, inc=1, device_id={"seq": lax.rem(me + k, seq)}, device_id_type=MESH
        )
    for k in range(1, slates):
        pl.semaphore_signal(
            barrier, inc=1, device_id={"slate": lax.rem(my_slate + k, slates)}, device_id_type=MESH
        )

    for t in range(3):
        tile = slice(t * third, (t + 1) * third)
        hidden = features_ref[tile].astype(f32) + personal_ref[...].astype(f32)
        x_ref[0, tile] = (hidden * rms_scale(hidden) * gain_in_ref[...]).astype(bf16)

    copies = {}

    def piece(group, part):
        return x_ref.at[group, part * third : (part + 1) * third]

    def copy(name, source, target, device):
        index = len(copies)
        copies[name] = pltpu.make_async_remote_copy(
            src_ref=source,
            dst_ref=target,
            send_sem=send_sem.at[index],
            recv_sem=recv_sem.at[index],
            device_id={"seq": device},
            device_id_type=MESH,
        )

    copy("own", x_ref.at[0], x_ref.at[1], partner)
    for p in range(3):
        copy(f"a{p}", piece(0, p), piece(2 + p, 0), across)
        copy(f"l{p}", piece(0, p), piece(2 + p, 1), right)
        copy(f"r{p}", piece(0, p), piece(2 + p, 2), left)
        copy(f"al{p}", piece(2 + p, 0), piece(8 + p, 1), right)
        copy(f"ar{p}", piece(2 + p, 0), piece(8 + p, 2), left)
        if p != 1:
            copy(f"o{p}", piece(2 + p, 1), piece(8 + p, 0), right)
        else:
            copy(f"o{p}", piece(2 + p, 2), piece(8 + p, 0), left)
        copy(f"ao{p}", piece(8 + p, 0), piece(14, p), across)
        copy(f"m{p}", x_ref.at[2 + p], x_ref.at[5 + p], partner)
        copy(f"n{p}", x_ref.at[8 + p], x_ref.at[11 + p], partner)
    copy("last", x_ref.at[14], x_ref.at[15], partner)
    copy("swap", give_ref, att_ref.at[core], partner)

    def start(*names):
        for name in names:
            copies[name].start()

    def arrived(*names):
        for name in names:
            copies[name].wait_recv()

    pl.semaphore_wait(barrier, seq - 1 + slates - 1)
    start("own")
    for p in range(3):
        start(f"a{p}", f"l{p}", f"r{p}")

    columns = pl.ds(pl.multiple_of(core * half, half), half)
    wq_t = wq_ref[:, columns].T
    wvt_ref[...] = wv_ref[:, columns].T
    row = lax.broadcasted_iota(jnp.int32, (16, rows), 0)
    for head in range(4):
        vt_ref[head, 64:80, :] = jnp.where(row == 0, 1.0, 0.0).astype(bf16)
    o_ref[...] = jnp.zeros_like(o_ref)
    project_queries(x_ref[0], wq_t, qt_ref, 0)
    arrived("own")
    project_queries(x_ref[1], wq_t, qt_ref, rows)

    def group(g, carry):
        for p in range(3):

            @pl.when(g == 2 + p)
            def _():
                arrived(f"a{p}", f"l{p}", f"r{p}")
                start(f"al{p}", f"ar{p}", f"o{p}", f"m{p}")

            @pl.when(g == 5 + p)
            def _():
                arrived(f"m{p}")

            @pl.when(g == 7)
            def _():
                arrived(f"o{p}")
                start(f"ao{p}")

            @pl.when(g == 8 + p)
            def _():
                arrived(f"al{p}", f"ar{p}")
                start(f"n{p}")

            @pl.when(g == 11 + p)
            def _():
                arrived(f"n{p}")

        @pl.when(g == 14)
        def _():
            arrived("ao0", "ao1", "ao2")
            start("last")

        @pl.when(g == 15)
        def _():
            arrived("last")

        project_keys(x_ref[g], wk_ref[:, columns], k_ref)
        project_values(x_ref[g], wvt_ref[...], vt_ref)
        attend(k_ref, vt_ref, qt_ref, o_ref, range(4), range(qt_ref.shape[2] // BLOCK))
        return carry

    lax.fori_loop(0, seq, group, 0)

    def finished(head, first):
        span = slice(first, first + rows)
        return (o_ref[head, 0:64, span] / o_ref[head, 64:65, span]).astype(bf16)

    for head in range(4):
        give_ref[head * 64 : (head + 1) * 64] = finished(head, rows)
    start("swap")
    for head in range(4):
        att_ref[core, head * 64 : (head + 1) * 64] = finished(head, 0)
    arrived("swap")

    sums = [jnp.zeros((1, third), f32)] * 3
    for t in range(3):
        tile = slice(t * third, (t + 1) * third)
        hidden = features_ref[tile].astype(f32) + personal_ref[...].astype(f32)
        mixed = hidden
        for c in range(2):
            mixed = mixed + lax.dot_general(
                att_ref[c, :, tile],
                wo_ref[c * half : (c + 1) * half],
                (((0,), (0,)), ((), ())),
                preferred_element_type=f32,
            )
        mixed_ref[tile] = mixed.astype(bf16)
        scored = jnp.sum(
            mixed * rms_scale(mixed) * gain_out_ref[...] * w_score_ref[...], axis=-1, keepdims=True
        )
        scored = jnp.broadcast_to(scored, (third, 128)).T[0:1]
        scores_ref[:, tile] = scored
        weight = jnp.exp(labels_ref[:, tile].astype(f32))
        terms = (jnp.exp(scored), weight, weight * scored)
        sums = [total + term for total, term in zip(sums, terms)]

    def shared(tile, buffer, sends, recvs, axis, mine, count):
        buffer[mine] = tile
        sent = []
        for k in range(1, count):
            sent.append(
                pltpu.make_async_remote_copy(
                    src_ref=buffer.at[mine],
                    dst_ref=buffer.at[mine],
                    send_sem=sends.at[k],
                    recv_sem=recvs.at[mine],
                    device_id={axis: lax.rem(mine + k, count)},
                    device_id_type=MESH,
                )
            )
            sent[-1].start()
        for k in range(1, count):
            other = lax.rem(mine + k, count)
            pltpu.make_async_remote_copy(
                src_ref=buffer.at[other],
                dst_ref=buffer.at[other],
                send_sem=sends.at[k],
                recv_sem=recvs.at[other],
                device_id={axis: other},
                device_id_type=MESH,
            ).wait_recv()
        total = buffer[0]
        for k in range(1, count):
            total = total + buffer[k]
        for one in sent:
            one.wait_send()
        return total

    row = lax.broadcasted_iota(jnp.int32, (8, 128), 0)
    tile = jnp.zeros((8, 128), f32)
    for i, total in enumerate(sums):
        tile = jnp.where(row == i, jnp.sum(total, axis=-1, keepdims=True), tile)
    tile = shared(tile, parts_ref, parts_send, parts_recv, "seq", me, seq)
    slate_loss = jnp.log(tile[0:1] / float(rows * seq)) - tile[2:3] / tile[1:2]
    slate_loss = jnp.broadcast_to(slate_loss, (8, 128))
    loss_ref[...] = shared(
        slate_loss, losses_ref, losses_send, losses_recv, "slate", my_slate, slates
    )
    for one in copies.values():
        one.wait_send()


def shards(
    features,
    user_ids,
    labels,
    user_table,
    gain_in,
    w_query,
    w_key,
    w_value,
    w_out,
    gain_out,
    w_score,
):
    _, rows, width = features.shape
    seq, slates = lax.axis_size("seq"), lax.axis_size("slate")
    personal = lax.dynamic_slice_in_dim(user_table, user_ids[0], 1, 0)
    vmem = pl.BlockSpec(memory_space=pltpu.VMEM)
    mixed, scores, loss = pl.pallas_call(
        functools.partial(fused_kernel, seq, slates),
        out_shape=(
            jax.ShapeDtypeStruct((rows, width), bf16),
            jax.ShapeDtypeStruct((1, rows), f32),
            jax.ShapeDtypeStruct((8, 128), f32),
        ),
        in_specs=[vmem] * 10,
        out_specs=(vmem, vmem, vmem),
        scratch_shapes=[
            pltpu.VMEM((seq, rows, width), bf16),
            pltpu.VMEM((2, rows, 128), bf16),
            pltpu.VMEM((4, 80, rows), bf16),
            pltpu.VMEM((4, 128, 2 * rows), bf16),
            pltpu.VMEM((4, 80, 2 * rows), f32),
            pltpu.VMEM((width // 2, rows), bf16),
            pltpu.VMEM((2, width // 2, rows), bf16),
            pltpu.VMEM((width // 2, width), bf16),
            pltpu.VMEM((seq, 8, 128), f32),
            pltpu.VMEM((slates, 8, 128), f32),
            pltpu.SemaphoreType.DMA((30,)),
            pltpu.SemaphoreType.DMA((30,)),
            pltpu.SemaphoreType.DMA((seq,)),
            pltpu.SemaphoreType.DMA((seq,)),
            pltpu.SemaphoreType.DMA((slates,)),
            pltpu.SemaphoreType.DMA((slates,)),
        ],
        compiler_params=pltpu.CompilerParams(
            collective_id=0, has_side_effects=True, vmem_limit_bytes=56 * 2**20
        ),
        name="slate_attention",
    )(
        features[0],
        personal,
        labels,
        gain_in[None],
        w_query,
        w_key,
        w_value,
        w_out,
        gain_out[None],
        w_score[None],
    )
    return (mixed[None], scores, loss[0, 0])


def solution(mesh):
    return jax.shard_map(
        shards,
        mesh=mesh,
        in_specs=(
            P("slate", "seq", None),
            P("slate"),
            P("slate", "seq"),
            P(),
            P(),
            P(),
            P(),
            P(),
            P(),
            P(),
            P(),
        ),
        out_specs=(P("slate", "seq", None), P("slate", "seq"), P()),
        check_vma=False,
    )
```

time: 229 us -> 130 us (0.57)
  waiting for transfers between devices: 79.4 us -> 0 us
  Pallas kernels: 97.6 us -> 124 us
  between operations: 16.9 us -> 1.39 us
  blocking collectives: 14.1 us -> 0 us
  other arithmetic: 9.79 us -> 0 us
  starting transfers between devices: 5.33 us -> 0 us
    all_gather x1 -> x0, waiting for transfers between devices: 73.5 us -> none  [shards(): segment = lax.all_gather(normed, 'seq', axis=0, tiled=True)]
    pallas_call x1, Pallas kernels: 97.6 us -> 124 us  [shards(): pl.pallas_call(functools.partial(fused_kernel, seq, slates), out_shape=(j...]
    all_to_all x1 -> x0, blocking collectives: 14.1 us -> none  [sent_to_all(): return lax.all_to_all(copies, axis, split_axis=0, concat_axis=0, tiled=True)]
    all_to_all x1 -> x0, waiting for transfers between devices: 5.35 us -> none  [sent_to_all(): return lax.all_to_all(copies, axis, split_axis=0, concat_axis=0, tiled=True)]
    all_to_all x1 -> x0, starting transfers between devices: 4.97 us -> none  [sent_to_all(): return lax.all_to_all(copies, axis, split_axis=0, concat_axis=0, tiled=True)]
    reduce_sum x6 -> x0, other arithmetic: 4.75 us -> none  [the longest x1 1.49 us: rms_norm(): jnp.mean(inputs_row * inputs_row, axis=-1, keepdims=True) + norm_eps]
  transfers between devices with their start and end apart: 3 -> 0, of which waited for: 3 -> 0; matrix products, arithmetic and copies ran while one was open for 1% -> 0% of each run, Pallas kernels for 0% -> 0%
where the time goes in v2:
time: 130 us
  Pallas kernels  124 us (95%)
  local copies, waits for them, and re-layouts  4.92 us (4%)
  between operations  1.39 us (1%)
    pallas_call x1, Pallas kernels, shards(): pl.pallas_call(functools.partial(fused_kernel, seq, slates), out_shape=(j...  124 us
    unnamed x6, local copies, waits for them, and re-layouts  3.15 us

profile of v2, /device:TPU:0, one launch (start us, length us, event | category | flops | bytes accessed | tf_op | source)
XLA Modules:
  0.0 130.1 jit_solution(11168102594561381730)
XLA Ops:
  0.6 0.0 copy-start
  1.4 0.5 copy-done
  1.9 0.6 constant_dynamic-slice_fusion.personal_ref
  2.5 123.8 %slate_attention.1 = (bf16[768,512]{1,0:T(8,128)(2,1)}, f32[1,768]{1,0:T(1,128)}, f32[8,128]{1,0:T(8,128)}) custom-call(bf16[768,512]{1,0:T(8,128)(2,1)} %bitcast.11, bf16[1,512]{1,0:T(2,128)(2,1)} %constant_dynamic-slice_fusion.personal_ref, s32[1,768]{1,0:T(1,128)} %labels_ref.1, f32[1,512]{1,0:T(1,128)} %bitcast.12, bf16[512,512]{1,0:T(8,128)(2,1)} %wq_ref.1, ...), custom_call_target="tpu_custom_call" | custom-call | tf_op jit(solution)/shard_map/slate_attention/pallas_call | solution.py:335
  126.3 1.2 slice.3
  127.5 0.0 copy-start.1
  127.5 2.1 %copy.17 = bf16[1,768,512]{2,1,0:T(8,128)(2,1)} copy(bf16[1,768,512]{2,1,0:T(8,128)(2,1)} %bitcast.10) | data formatting | bytes 1572864
  129.6 0.0 copy-done.1
  129.6 0.6 copy.18
Async XLA Ops:
  0.6 1.2 copy-start
  127.5 2.1 %copy-start.1 = (f32[1,768]{1,0:T(1,128)S(1)}, f32[1,768]{1,0:T(1,128)}, u32[]{:S(2)}) copy-start(f32[1,768]{1,0:T(1,128)} %get-tuple-element.13) | copy-start | bytes 9220

commit v3 on v2

--- a/solution.py
+++ b/solution.py
@@ -47,24 +47,24 @@
         qt_ref[head, other : other + 64, at : at + count] = jnp.zeros((64, count), bf16)
 
 
-def attend(k_ref, vt_ref, qt_ref, o_ref, heads, tiles):
-    kts = k_ref.shape[1] // BLOCK
-    work = [(h, t, b) for h in heads for t in tiles for b in range(kts)]
+def attend(k_refs, vt_refs, qt_ref, o_ref, heads, tiles):
+    kts = k_refs[0].shape[1] // BLOCK
+    work = [(g, h, t, b) for g in range(2) for h in heads for t in tiles for b in range(kts)]
     ready = {}
     total = None
     for i in range(len(work) + AHEAD):
         if i < len(work):
-            h, t, b = work[i]
+            g, h, t, b = work[i]
             products = jnp.dot(
-                k_ref[h // 2, b * BLOCK : (b + 1) * BLOCK],
+                k_refs[g][h // 2, b * BLOCK : (b + 1) * BLOCK],
                 qt_ref[h, :, t * BLOCK : (t + 1) * BLOCK],
                 preferred_element_type=f32,
             )
             ready[i] = capped_weight(products).astype(bf16)
         if i >= AHEAD:
-            h, t, b = work[i - AHEAD]
+            g, h, t, b = work[i - AHEAD]
             part = jnp.dot(
-                vt_ref[h, :, b * BLOCK : (b + 1) * BLOCK],
+                vt_refs[g][h, :, b * BLOCK : (b + 1) * BLOCK],
                 ready.pop(i - AHEAD),
                 preferred_element_type=f32,
             )
@@ -94,8 +94,10 @@
     scores_ref,
     loss_ref,
     x_ref,
-    k_ref,
-    vt_ref,
+    k_a_ref,
+    k_b_ref,
+    vt_a_ref,
+    vt_b_ref,
     qt_ref,
     o_ref,
     give_ref,
@@ -187,58 +189,67 @@
     wq_t = wq_ref[:, columns].T
     wvt_ref[...] = wv_ref[:, columns].T
     row = lax.broadcasted_iota(jnp.int32, (16, rows), 0)
-    for head in range(4):
+    k_refs, vt_refs = (k_a_ref, k_b_ref), (vt_a_ref, vt_b_ref)
+    for vt_ref, head in [(v, h) for v in vt_refs for h in range(4)]:
         vt_ref[head, 64:80, :] = jnp.where(row == 0, 1.0, 0.0).astype(bf16)
     o_ref[...] = jnp.zeros_like(o_ref)
     project_queries(x_ref[0], wq_t, qt_ref, 0)
     arrived("own")
     project_queries(x_ref[1], wq_t, qt_ref, rows)
 
-    def group(g, carry):
-        for p in range(3):
-
-            @pl.when(g == 2 + p)
-            def _():
+    def pair(i, carry):
+        @pl.when(i == 1)
+        def _():
+            for p in (0, 1):
                 arrived(f"a{p}", f"l{p}", f"r{p}")
                 start(f"al{p}", f"ar{p}", f"o{p}", f"m{p}")
 
-            @pl.when(g == 5 + p)
-            def _():
-                arrived(f"m{p}")
-
-            @pl.when(g == 7)
-            def _():
+        @pl.when(i == 2)
+        def _():
+            arrived("a2", "l2", "r2", "m0")
+            start("al2", "ar2", "o2", "m2")
+
+        @pl.when(i == 3)
+        def _():
+            arrived("m1", "m2")
+            for p in (0, 1):
                 arrived(f"o{p}")
                 start(f"ao{p}")
 
-            @pl.when(g == 8 + p)
-            def _():
+        @pl.when(i == 4)
+        def _():
+            for p in (0, 1):
                 arrived(f"al{p}", f"ar{p}")
                 start(f"n{p}")
-
-            @pl.when(g == 11 + p)
-            def _():
-                arrived(f"n{p}")
-
-        @pl.when(g == 14)
-        def _():
-            arrived("ao0", "ao1", "ao2")
+            arrived("o2")
+            start("ao2")
+
+        @pl.when(i == 5)
+        def _():
+            arrived("al2", "ar2", "n0")
+            start("n2")
+
+        @pl.when(i == 6)
+        def _():
+            arrived("n1", "n2", "ao0", "ao1", "ao2")
             start("last")
 
-        @pl.when(g == 15)
+        @pl.when(i == 7)
         def _():
             arrived("last")
 
-        project_keys(x_ref[g], wk_ref[:, columns], k_ref)
-        project_values(x_ref[g], wvt_ref[...], vt_ref)
-        attend(k_ref, vt_ref, qt_ref, o_ref, range(4), range(qt_ref.shape[2] // BLOCK))
+        for b in range(2):
+            project_keys(x_ref[2 * i + b], wk_ref[:, columns], k_refs[b])
+            project_values(x_ref[2 * i + b], wvt_ref[...], vt_refs[b])
+        tiles = range(qt_ref.shape[2] // BLOCK)
+        attend(k_refs, vt_refs, qt_ref, o_ref, range(4), tiles)
         return carry
 
-    lax.fori_loop(0, seq, group, 0)
+    lax.fori_loop(0, seq // 2, pair, 0)
 
     def finished(head, first):
         span = slice(first, first + rows)
-        return (o_ref[head, 0:64, span] / o_ref[head, 64:65, span]).astype(bf16)
+        return (o_ref[head, 0:64, span] * (1.0 / o_ref[head, 64:65, span])).astype(bf16)
 
     for head in range(4):
         give_ref[head * 64 : (head + 1) * 64] = finished(head, rows)
@@ -310,7 +321,7 @@
     slate_loss = jnp.broadcast_to(slate_loss, (8, 128))
     loss_ref[...] = shared(
         slate_loss, losses_ref, losses_send, losses_recv, "slate", my_slate, slates
-    )
+    )[0:1, 0:1]
     for one in copies.values():
         one.wait_send()
 
@@ -335,15 +346,17 @@
     mixed, scores, loss = pl.pallas_call(
         functools.partial(fused_kernel, seq, slates),
         out_shape=(
-            jax.ShapeDtypeStruct((rows, width), bf16),
-            jax.ShapeDtypeStruct((1, rows), f32),
-            jax.ShapeDtypeStruct((8, 128), f32),
+            pltpu.VMEM((rows, width), bf16),
+            pltpu.VMEM((1, rows), f32),
+            jax.ShapeDtypeStruct((1, 1), f32),
         ),
         in_specs=[vmem] * 10,
         out_specs=(vmem, vmem, vmem),
         scratch_shapes=[
             pltpu.VMEM((seq, rows, width), bf16),
             pltpu.VMEM((2, rows, 128), bf16),
+            pltpu.VMEM((2, rows, 128), bf16),
+            pltpu.VMEM((4, 80, rows), bf16),
             pltpu.VMEM((4, 80, rows), bf16),
             pltpu.VMEM((4, 128, 2 * rows), bf16),
             pltpu.VMEM((4, 80, 2 * rows), f32),

time: 130 us -> 124 us (0.954)
  Pallas kernels: 124 us -> 118 us
  local copies, waits for them, and re-layouts: 4.92 us -> 2.55 us
  between operations: 1.39 us -> 3.15 us
    pallas_call x1, Pallas kernels: 124 us -> 118 us  [shards(): pl.pallas_call(functools.partial(fused_kernel, seq, slates), out_shape=(p...]
    unnamed x6 -> x4, local copies, waits for them, and re-layouts: 3.15 us -> 1.96 us
where the time goes in v3:
time: 124 us
  Pallas kernels  118 us (95%)
  between operations  3.15 us (3%)
  local copies, waits for them, and re-layouts  2.55 us (2%)
    pallas_call x1, Pallas kernels, shards(): pl.pallas_call(functools.partial(fused_kernel, seq, slates), out_shape=(p...  118 us

profile of v3, /device:TPU:0, one launch (start us, length us, event | category | flops | bytes accessed | tf_op | source)
XLA Modules:
  0.0 123.9 jit_solution(16039389541261684503)
XLA Ops:
  0.6 0.0 copy-start
  1.4 0.5 copy-done
  1.9 0.6 constant_dynamic-slice_fusion.personal_ref
  2.5 118.2 %slate_attention.1 = (bf16[768,512]{1,0:T(8,128)(2,1)S(1)}, f32[1,768]{1,0:T(1,128)S(1)}, f32[1,1]{1,0:T(1,128)}) custom-call(bf16[768,512]{1,0:T(8,128)(2,1)} %bitcast.11, bf16[1,512]{1,0:T(2,128)(2,1)} %constant_dynamic-slice_fusion.personal_ref, s32[1,768]{1,0:T(1,128)} %labels_ref.1, f32[1,512]{1,0:T(1,128)} %bitcast.12, bf16[512,512]{1,0:T(8,128)(2,1)} %wq_ref.1, ...), custom_call_target="tpu_custom_call" | custom-call | tf_op jit(solution)/shard_map/slate_attention/pallas_call | solution.py:346
  120.6 0.9 copy.17
  121.5 0.6 copy.18
Async XLA Ops:
  0.6 1.2 %copy-start = (bf16[1024,512]{1,0:T(8,128)(2,1)S(1)}, bf16[1024,512]{1,0:T(8,128)(2,1)}, u32[]{:S(2)}) copy-start(bf16[1024,512]{1,0:T(8,128)(2,1)} %param.14) | copy-start | bytes 3145732
